TPU v7x, 16 devices: a whole 2x2x2 slice. The times are simulated.
16 devices in a mesh: dp: 4 (over z, y), ep: 4 (over x, core).
Axes of the slice: x: 2, y: 2, z: 2, core: 2. Of those that a mesh axis runs over, the one named last changes fastest.
Arguments:
- x_tok: bfloat16 [1024, 1536], P(('dp', 'ep')), parts along dimension 0
- topk_idx: int32 [1024, 6], P(('dp', 'ep')), parts along dimension 0
- topk_w: float32 [1024, 6], P(('dp', 'ep')), parts along dimension 0
- w_in: bfloat16 [64, 1536, 512], P('ep')
- w_out: bfloat16 [64, 512, 1536], P('ep')
- shared_in: bfloat16 [1536, 1024], replicated
- shared_out: bfloat16 [1024, 1536], replicated
Outputs:
- output: bfloat16 [1024, 1536], P(('dp', 'ep')), parts along dimension 0
There are 4 independent parts. A program takes and returns all parts, laid end to end along the dimension named above; an argument that names none is the same for every part.
All inputs are finite; a program needn't handle non-finite values.
Results may differ from a plain program's by a relative error of at most 0.001.
Values are sent between devices in bfloat16 or wider.
A program may use at most 1 GiB of HBM per device.

v0:
```python
import jax
import jax.numpy as jnp
from jax import lax
from jax.sharding import PartitionSpec as P

LOAD_MULT = 3


def slot_tables(topk_idx, topk_w, num_experts, slot_cap):
    tok_rows, top_k = topk_idx.shape
    expert_hot = (topk_idx[:, :, None] == jnp.arange(num_experts, dtype=jnp.int32)).astype(jnp.int32)
    running = jnp.cumsum(expert_hot.reshape(tok_rows * top_k, num_experts), axis=0)
    slot_pos = jnp.sum(running.reshape(tok_rows, top_k, num_experts) * expert_hot, axis=2) - 1
    slot_hot = (slot_pos[:, :, None] == jnp.arange(slot_cap, dtype=jnp.int32)).astype(jnp.bfloat16)
    gate_hot = expert_hot.astype(jnp.bfloat16) * topk_w.astype(jnp.bfloat16)[:, :, None]
    combine = jnp.einsum('tje,tjc->tec', gate_hot, slot_hot, preferred_element_type=jnp.float32).astype(jnp.bfloat16)
    dispatch = (combine != 0).astype(jnp.bfloat16)
    return combine, dispatch


def solution(mesh):
    group_size = mesh.shape['ep']

    def local_layer(x_loc, idx_loc, gate_loc, w_in, w_out, shared_in, shared_out):
        tok_rows, top_k = idx_loc.shape
        num_experts = w_in.shape[0] * group_size
        slot_cap = min(tok_rows, LOAD_MULT * tok_rows * top_k // num_experts)
        combine, dispatch = slot_tables(idx_loc, gate_loc, num_experts, slot_cap)
        send_rows = jnp.einsum('tec,tm->ecm', dispatch, x_loc, preferred_element_type=jnp.float32).astype(jnp.bfloat16)
        recv_rows = lax.all_to_all(send_rows, 'ep', 0, 1, tiled=True)
        hidden = jax.nn.gelu(jnp.einsum('erm,emf->erf', recv_rows, w_in, preferred_element_type=jnp.float32), approximate=True).astype(jnp.bfloat16)
        expert_out = jnp.einsum('erf,efm->erm', hidden, w_out, preferred_element_type=jnp.float32).astype(jnp.bfloat16)
        back_rows = lax.all_to_all(expert_out, 'ep', 1, 0, tiled=True)
        routed = jnp.einsum('tec,ecm->tm', combine, back_rows, preferred_element_type=jnp.float32)
        shared_hidden = jax.nn.gelu(jnp.dot(x_loc, shared_in, preferred_element_type=jnp.float32), approximate=True).astype(jnp.bfloat16)
        shared_val = jnp.dot(shared_hidden, shared_out, preferred_element_type=jnp.float32)
        return (routed + shared_val).astype(jnp.bfloat16)

    tok_spec = P(('dp', 'ep'), None)
    expert_spec = P('ep', None, None)
    whole_spec = P(None, None)
    return jax.shard_map(local_layer, mesh=mesh, in_specs=(tok_spec, tok_spec, tok_spec, expert_spec, expert_spec, whole_spec, whole_spec), out_specs=tok_spec, check_vma=False)
```

profile of v0, /device:TPU:0, one launch (start us, length us, event | category | flops | bytes accessed | tf_op | source)
XLA Modules:
  0.0 148.7 jit_solution(5865065588632827578)
XLA Ops:
  0.0 0.0 copy-start
  0.0 0.9 copy.49
  0.9 0.1 eq.53
  1.1 0.1 eq.49
  1.2 0.7 convert_element_type.36
  1.9 0.1 copy.50
  2.0 0.9 reduce-window.6
  2.9 0.2 slice_reduce_fusion
  3.2 0.1 fusion.42
  3.3 0.1 sub.7
  3.5 0.8 fusion.29
  4.3 0.7 copy-done.1
  5.0 2.1 %convolution_convert_fusion.1 = bf16[64,18,1536]{2,0,1:T(8,128)(2,1)S(1)} fusion(bf16[64,1536]{1,0:T(8,128)(2,1)} %param.7, bf16[64,64,18]{1,2,0:T(8,128)(2,1)S(1)} %fusion.29), kind=kOutput, calls=%fused_computation.1 | convolution fusion | flops 228335616 | bytes 3883008 | tf_op jit(solution)/shard_map/tec,tm->ecm/dot_general | solution.py:29
  7.1 2.0 %copy.56 = bf16[64,18,1536]{2,1,0:T(8,128)(2,1)S(1)} copy(bf16[64,18,1536]{2,0,1:T(8,128)(2,1)S(1)} %convolution_convert_fusion.1) | data formatting | bytes 7077888 | tf_op jit(solution)/shard_map/convert_element_type | solution.py:29
  9.1 58.1 %all_to_all.36 = bf16[64,18,1536]{2,1,0:T(8,128)(2,1)S(1)} all-to-all(bf16[64,18,1536]{2,1,0:T(8,128)(2,1)S(1)} %copy.56), channel_id=1, replica_groups=mesh['dp'=4,'ep'=4] {'ep'}, dimensions={0} | all-to-all | bytes 7077888 | tf_op jit(solution)/shard_map/all_to_all | solution.py:30
  67.1 2.9 %copy.58 = bf16[16,4,18,1536]{3,0,2,1:T(8,128)(2,1)} copy(bf16[16,4,18,1536]{3,2,0,1:T(8,128)(2,1)S(1)} %bitcast.35) | data formatting | bytes 7077888 | tf_op jit(solution)/shard_map/all_to_all | solution.py:30
  70.0 26.2 %convolution_convert_fusion = bf16[16,72,1536]{2,1,0:T(8,128)(2,1)} fusion(bf16[16,512,1536]{2,1,0:T(8,128)(2,1)} %param.11, bf16[16,1536,512]{2,1,0:T(8,128)(2,1)} %param.10, bf16[16,72,1536]{2,0,1:T(8,128)(2,1)} %bitcast.36), kind=kOutput, calls=%fused_computation | convolution fusion | flops 3630956544 | bytes 57409536 | tf_op jit(solution)/shard_map/erf,efm->erm/dot_general | solution.py:32
  96.2 3.1 %copy.60 = bf16[16,72,1536]{2,0,1:T(8,128)(2,1)S(1)} copy(bf16[16,72,1536]{2,1,0:T(8,128)(2,1)} %convolution_convert_fusion) | data formatting | bytes 7077888 | tf_op jit(solution)/shard_map/convert_element_type | solution.py:32
  99.3 43.6 %all_to_all.37 = bf16[16,72,1536]{2,0,1:T(8,128)(2,1)S(1)} all-to-all(bf16[16,72,1536]{2,0,1:T(8,128)(2,1)S(1)} %copy.60), channel_id=1, replica_groups=mesh['dp'=4,'ep'=4] {'ep'}, dimensions={1} | all-to-all | bytes 7077888 | tf_op jit(solution)/shard_map/all_to_all | solution.py:33
  143.0 0.3 copy.61
  143.3 0.7 copy-done.2
  144.0 0.8 convolution_bitcast_fusion
  144.7 0.0 copy-done
  144.7 3.9 %fusion.10 = bf16[64,1536]{1,0:T(8,128)(2,1)} fusion(f32[64,1536]{1,0:T(8,128)S(1)} %convolution_bitcast_fusion, bf16[1024,1536]{1,0:T(8,128)(2,1)S(1)} %copy-done, bf16[64,1536]{1,0:T(8,128)(2,1)} %param.7, bf16[1536,1024]{1,0:T(8,128)(2,1)} %param.12), kind=kOutput, calls=%fused_computation.15 | convolution fusion | flops 403439616 | bytes 7077888 | tf_op jit(solution)/shard_map/dot_general | solution.py:36
  (5 shorter events, 0.1 us)
Async XLA Ops:
  0.0 144.7 %copy-start = (bf16[1024,1536]{1,0:T(8,128)(2,1)S(1)}, bf16[1024,1536]{1,0:T(8,128)(2,1)}, u32[]{:S(2)}) copy-start(bf16[1024,1536]{1,0:T(8,128)(2,1)} %param.13) | copy-start | bytes 9437188
  4.3 0.8 copy-start.1
  143.0 1.0 copy-start.2
where the time goes:
time: 149 us
  blocking collectives  102 us (68%)
  matrix products  33.8 us (23%)
  local copies, waits for them, and re-layouts  11.3 us (8%)
  other arithmetic  1.77 us (1%)
    all_to_all x1, blocking collectives, local_layer(): recv_rows = lax.all_to_all(send_rows, 'ep', 0, 1, tiled=True)  58.1 us
    all_to_all x1, blocking collectives, local_layer(): back_rows = lax.all_to_all(expert_out, 'ep', 1, 0, tiled=True)  43.6 us
    dot_general x1, matrix products, local_layer(): jnp.einsum('erf,efm->erm', hidden, w_out, preferred_element_type=jnp.floa...  26.2 us
    dot_general x1, matrix products, local_layer(): jnp.dot(shared_hidden, shared_out, preferred_element_type=jnp.float32)  3.95 us
    convert_element_type x1, local copies, waits for them, and re-layouts, local_layer(): jnp.einsum('erf,efm->erm', hidden, w_out, preferred_element_type=jnp.floa...  3.06 us

commit v1 on v0

v1 whole, which is shorter than its diff:
```python
import functools
import math

import jax
import jax.numpy as jnp
from jax import lax
from jax.experimental import pallas as pl
from jax.experimental.pallas import tpu as pltpu
from jax.sharding import PartitionSpec as P

MESH = pl.DeviceIdType.MESH
LOAD_MULT = 3
COLS = 256
GELU_A = math.sqrt(2.0 / math.pi)
GELU_B = GELU_A * 0.044715


def gelu(z):
    return 0.5 * z * (1.0 + jnp.tanh(z * (GELU_A + GELU_B * (z * z))))


def dot(a, b):
    return jnp.dot(a, b, preferred_element_type=jnp.float32)


def layer_kernel(
    dims,
    x_hbm, idx_hbm, gate_hbm, win_hbm, wout_hbm, sin_hbm, sout_hbm,
    y_hbm,
    x_all, win, wout, idx_all, gate_all, disp, comb, rows_in, acc, hidden, rows_out,
    part, sib_part, sib_fwd, link_out, link_in, y_buf, shared_h, shared_u,
    small_sem, x_sem, win_sem, wout_sem, shared_sem, y_sem,
    meta_send, meta_recv, xl_send, xl_recv, xs_send, xs_recv, xf_send, xf_recv,
    ps_send, ps_recv, pf_send, pf_recv, pl_send, pl_recv,
):
    tok, top_k, local_e, slot, tokens = dims
    d_model, ff = win_hbm.shape[1], win_hbm.shape[2]
    chunks = d_model // COLS
    me = lax.axis_index('ep')
    chip, core = lax.div(me, 2), lax.rem(me, 2)
    sib = chip * 2 + (1 - core)
    mir = (1 - chip) * 2 + core
    diag = (1 - chip) * 2 + (1 - core)
    peers = (sib, mir, diag)

    def rows_of(dev):
        return pl.ds(pl.multiple_of(dev * tok, tok), tok)

    def remote(src, dst, send, recv, dev):
        return pltpu.make_async_remote_copy(
            src_ref=src, dst_ref=dst, send_sem=send, recv_sem=recv,
            device_id={'ep': dev}, device_id_type=MESH)

    idx_cp = pltpu.make_async_copy(idx_hbm, idx_all.at[me], small_sem.at[0])
    gate_cp = pltpu.make_async_copy(gate_hbm, gate_all.at[me], small_sem.at[1])
    idx_cp.start()
    gate_cp.start()
    x_cps = [pltpu.make_async_copy(x_hbm.at[:, pl.ds(k * COLS, COLS)], x_all.at[k, rows_of(me)], x_sem.at[k]) for k in range(chunks)]
    for cp in x_cps:
        cp.start()
    win_cps = [pltpu.make_async_copy(win_hbm.at[:, pl.ds(k * COLS, COLS), :], win.at[k], win_sem.at[k]) for k in range(chunks)]
    for cp in win_cps:
        cp.start()
    wout_cps = [pltpu.make_async_copy(wout_hbm.at[:, :, pl.ds(n * COLS, COLS)], wout.at[n], wout_sem.at[n]) for n in range(chunks)]
    for cp in wout_cps:
        cp.start()

    barrier = pltpu.get_barrier_semaphore()
    for peer in peers:
        pl.semaphore_signal(barrier, inc=1, device_id={'ep': peer}, device_id_type=MESH)

    idx_cp.wait()
    gate_cp.wait()
    pl.semaphore_wait(barrier, 3)
    meta_cps = []
    for r, peer in enumerate(peers):
        meta_cps.append(remote(idx_all.at[me], idx_all.at[me], meta_send.at[r], meta_recv.at[r], peer))
        meta_cps.append(remote(gate_all.at[me], gate_all.at[me], meta_send.at[3 + r], meta_recv.at[3 + r], peer))
    for cp in meta_cps:
        cp.start()
    xl_cps, xs_cps, xf_cps = [], [], []
    for k in range(chunks):
        mine, theirs = x_all.at[k, rows_of(me)], x_all.at[k, rows_of(mir)]
        xl_cps.append(remote(mine, mine, xl_send.at[k], xl_recv.at[k], mir))
        xs_cps.append(remote(mine, mine, xs_send.at[k], xs_recv.at[k], sib))
        xf_cps.append(remote(theirs, theirs, xf_send.at[k], xf_recv.at[k], sib))
    for k in range(chunks):
        x_cps[k].wait()
        xl_cps[k].start()
        xs_cps[k].start()

    for cp in meta_cps:
        cp.wait_recv()
    group = tokens // tok
    idx_t = jnp.concatenate([idx_all[s] for s in range(group)], axis=1)
    gate_t = jnp.concatenate([gate_all[s] for s in range(group)], axis=1).astype(jnp.bfloat16).astype(jnp.float32)
    expert_id = lax.broadcasted_iota(jnp.int32, (local_e, tokens), 0) + me * local_e
    picked = jnp.zeros((local_e, tokens), jnp.float32)
    gates = jnp.zeros((local_e, tokens), jnp.float32)
    for j in range(top_k):
        hit = idx_t[j:j + 1, :] == expert_id
        picked = picked + jnp.where(hit, 1.0, 0.0)
        gates = gates + jnp.where(hit, gate_t[j:j + 1, :], 0.0)
    before = (lax.broadcasted_iota(jnp.int32, (tokens, tokens), 0) < lax.broadcasted_iota(jnp.int32, (tokens, tokens), 1))
    rank = dot(picked.astype(jnp.bfloat16), jnp.where(before, 1.0, 0.0).astype(jnp.bfloat16))
    rank = jnp.where(picked > 0.5, rank, -1.0)
    slot_id = lax.broadcasted_iota(jnp.int32, (slot, tokens), 0).astype(jnp.float32)
    for e in range(local_e):
        here = slot_id == rank[e:e + 1, :]
        disp[pl.ds(e * slot, slot), :] = jnp.where(here, 1.0, 0.0).astype(jnp.bfloat16)
        rows_out[pl.ds(e * slot, slot), :] = jnp.where(here, gates[e:e + 1, :], 0.0).astype(jnp.bfloat16)
    for i in range(local_e * slot // 256):
        comb[:, pl.ds(i * 256, 256)] = rows_out[pl.ds(i * 256, 256), :].T

    xl_cps[0].wait_recv()
    xf_cps[0].start()
    for k in range(chunks):
        if k + 1 < chunks:
            xl_cps[k + 1].wait_recv()
            xf_cps[k + 1].start()
        xs_cps[k].wait_recv()
        xf_cps[k].wait_recv()
        rows_in[...] = dot(disp[...], x_all[k]).astype(jnp.bfloat16)
        win_cps[k].wait()
        for e in range(local_e):
            r = pl.ds(e * slot, slot)
            term = dot(rows_in[r, :], win[k, e])
            if k == 0:
                acc[r, :] = term
            elif k + 1 < chunks:
                acc[r, :] = acc[r, :] + term
            else:
                hidden[r, :] = gelu(acc[r, :] + term).astype(jnp.bfloat16)

    shared_cps = []
    for k in range(chunks):
        for j in range(2):
            shared_cps.append(pltpu.make_async_copy(
                sin_hbm.at[pl.ds(k * COLS, COLS), pl.ds(j * ff, ff)], win.at[k, j], shared_sem.at[k * 2 + j]))
    for i in range(4):
        for j in range(3):
            shared_cps.append(pltpu.make_async_copy(
                sout_hbm.at[pl.ds(i * COLS, COLS), pl.ds(j * ff, ff)], win.at[i, 2 + j], shared_sem.at[12 + i * 3 + j]))
    for cp in shared_cps:
        cp.start()

    ps_cps = [remote(part.at[n, rows_of(sib)], sib_part.at[n], ps_send.at[n], ps_recv.at[n], sib) for n in range(chunks)]
    pf_cps = [remote(part.at[n, rows_of(diag)], sib_fwd.at[n], pf_send.at[n], pf_recv.at[n], sib) for n in range(chunks)]
    pl_cps = [remote(link_out.at[n], link_in.at[n], pl_send.at[n], pl_recv.at[n], mir) for n in range(chunks)]

    def send_back(n):
        pf_cps[n].wait_recv()
        link_out[n] = part[n, rows_of(mir), :] + sib_fwd[n]
        pl_cps[n].start()

    for n in range(chunks):
        wout_cps[n].wait()
        for e in range(local_e):
            r = pl.ds(e * slot, slot)
            rows_out[r, :] = dot(hidden[r, :], wout[n, e]).astype(jnp.bfloat16)
        part[n] = dot(comb[...], rows_out[...])
        pf_cps[n].start()
        ps_cps[n].start()
        if n:
            send_back(n - 1)
    send_back(chunks - 1)

    for cp in shared_cps:
        cp.wait()
    for j in range(2):
        s = dot(x_all[0, rows_of(me), :], win[0, j])
        for k in range(1, chunks):
            s = s + dot(x_all[k, rows_of(me), :], win[k, j])
        shared_h[:, pl.ds(j * ff, ff)] = gelu(s).astype(jnp.bfloat16)
    for j in range(3):
        u = dot(shared_h[:, 0:COLS], win[0, 2 + j])
        for i in range(1, 4):
            u = u + dot(shared_h[:, pl.ds(i * COLS, COLS)], win[i, 2 + j])
        shared_u[:, pl.ds(j * ff, ff)] = u

    y_cps = [pltpu.make_async_copy(y_buf.at[n], y_hbm.at[:, pl.ds(n * COLS, COLS)], y_sem.at[n]) for n in range(chunks)]
    for n in range(chunks):
        ps_cps[n].wait_recv()
        mine = shared_u[:, pl.ds(n * COLS, COLS)] + part[n, rows_of(me), :] + sib_part[n]
        pl_cps[n].wait_recv()
        y_buf[n] = (mine + link_in[n]).astype(jnp.bfloat16)
        y_cps[n].start()
    for cp in meta_cps + xl_cps + xs_cps + xf_cps + ps_cps + pf_cps + pl_cps:
        cp.wait_send()
    for cp in y_cps:
        cp.wait()


def solution(mesh):
    group = mesh.shape['ep']

    def local_layer(x_loc, idx_loc, gate_loc, w_in, w_out, shared_in, shared_out):
        tok, top_k = idx_loc.shape
        local_e, d_model, ff = w_in.shape
        fs = shared_in.shape[1]
        tokens = tok * group
        cap = min(tok, LOAD_MULT * tok * top_k // (local_e * group))
        slot = -(-cap * group // 16) * 16
        total = local_e * slot
        chunks = d_model // COLS
        bf16, f32 = jnp.bfloat16, jnp.float32
        dma = pltpu.SemaphoreType.DMA
        scratch = [
            pltpu.VMEM((chunks, tokens, COLS), bf16),
            pltpu.VMEM((chunks, local_e, COLS, ff), bf16),
            pltpu.VMEM((chunks, local_e, ff, COLS), bf16),
            pltpu.VMEM((group, top_k, tok), jnp.int32),
            pltpu.VMEM((group, top_k, tok), f32),
            pltpu.VMEM((total, tokens), bf16),
            pltpu.VMEM((tokens, total), bf16),
            pltpu.VMEM((total, COLS), bf16),
            pltpu.VMEM((total, ff), f32),
            pltpu.VMEM((total, ff), bf16),
            pltpu.VMEM((total, COLS), bf16),
            pltpu.VMEM((chunks, tokens, COLS), f32),
            pltpu.VMEM((chunks, tok, COLS), f32),
            pltpu.VMEM((chunks, tok, COLS), f32),
            pltpu.VMEM((chunks, tok, COLS), f32),
            pltpu.VMEM((chunks, tok, COLS), f32),
            pltpu.VMEM((chunks, tok, COLS), bf16),
            pltpu.VMEM((tok, fs), bf16),
            pltpu.VMEM((tok, d_model), f32),
            dma((2,)), dma((chunks,)), dma((chunks,)), dma((chunks,)), dma((24,)), dma((chunks,)),
            dma((6,)), dma((6,)),
        ] + [dma((chunks,))] * 12
        any_spec = pl.BlockSpec(memory_space=pl.ANY)
        return pl.pallas_call(
            functools.partial(layer_kernel, (tok, top_k, local_e, slot, tokens)),
            out_shape=jax.ShapeDtypeStruct((tok, d_model), bf16),
            in_specs=[any_spec] * 7,
            out_specs=any_spec,
            scratch_shapes=scratch,
            compiler_params=pltpu.CompilerParams(
                collective_id=0, has_side_effects=True, vmem_limit_bytes=67043328),
        )(x_loc, idx_loc.T, gate_loc.T, w_in, w_out, shared_in, shared_out)

    tok_spec = P(('dp', 'ep'), None)
    expert_spec = P('ep', None, None)
    whole_spec = P(None, None)
    return jax.shard_map(
        local_layer, mesh=mesh,
        in_specs=(tok_spec, tok_spec, tok_spec, expert_spec, expert_spec, whole_spec, whole_spec),
        out_specs=tok_spec, check_vma=False)
```

time: 149 us -> 42.5 us (0.29)
  blocking collectives: 102 us -> 0 us
  Pallas kernels: 0 us -> 40.7 us
  matrix products: 33.8 us -> 0 us
  local copies, waits for them, and re-layouts: 11.3 us -> 1.62 us
  other arithmetic: 1.77 us -> 0 us
    all_to_all x2 -> x0, blocking collectives: 102 us -> none  [the longest x1 58.1 us: local_layer(): recv_rows = lax.all_to_all(send_rows, 'ep', 0, 1, tiled=True)]
    pallas_call x0 -> x1, Pallas kernels: none -> 40.7 us  [local_layer(): pl.pallas_call(functools.partial(layer_kernel, (tok, top_k, local_e, slot...]
    dot_general x5 -> x0, matrix products: 33.8 us -> none  [the longest x1 26.2 us: local_layer(): jnp.einsum('erf,efm->erm', hidden, w_out, preferred_element_type=jnp.floa...]
    convert_element_type x3 -> x0, local copies, waits for them, and re-layouts: 5.16 us -> none  [the longest x1 3.06 us: local_layer(): jnp.einsum('erf,efm->erm', hidden, w_out, preferred_element_type=jnp.floa...]
    all_to_all x2 -> x0, local copies, waits for them, and re-layouts: 3.19 us -> none  [the longest x1 2.88 us: local_layer(): recv_rows = lax.all_to_all(send_rows, 'ep', 0, 1, tiled=True)]
where the time goes in v1:
time: 42.5 us; the launch traced here: 42.3 us
  Pallas kernels  40.7 us (96%)
  local copies, waits for them, and re-layouts  1.62 us (4%)
    pallas_call x1, Pallas kernels, local_layer(): pl.pallas_call(functools.partial(layer_kernel, (tok, top_k, local_e, slot...  40.7 us
    unnamed x1, local copies, waits for them, and re-layouts  1.62 us

profile of v1, /device:TPU:0, one launch (start us, length us, event | category | flops | bytes accessed | tf_op | source)
XLA Modules:
  0.0 42.3 jit_solution(9762419505319247074)
XLA Ops:
  0.0 40.7 %shard_map.73 = bf16[64,1536]{1,0:T(8,128)(2,1)} custom-call(bf16[64,1536]{1,0:T(8,128)(2,1)} %x_hbm.1, s32[6,64]{1,0:T(8,128)} %bitcast.2, f32[6,64]{1,0:T(8,128)} %bitcast.3, bf16[16,1536,512]{2,1,0:T(8,128)(2,1)} %win_hbm.1, bf16[16,512,1536]{2,1,0:T(8,128)(2,1)} %wout_hbm.1, bf16[1536,1024]{1,0:T(8,128)(2,1)} %sin_hbm.1, bf16[1024,1536]{1,0:T(8,128)(2,1)} %sout_hbm.1), custom_call_target="tpu_custom_call" | custom-call | tf_op jit(solution)/shard_map/pallas_call | solution.py:232
  40.7 1.6 %copy.9 = bf16[64,1536]{1,0:T(8,128)(2,1)} copy(bf16[64,1536]{1,0:T(8,128)(2,1)} %shard_map.73) | data formatting | bytes 393216

commit v2 on v1

--- a/solution.py
+++ b/solution.py
@@ -10,6 +10,8 @@
 
 MESH = pl.DeviceIdType.MESH
 LOAD_MULT = 3
+VMEM_LIMIT = 61500000
+scope = jax.named_scope
 COLS = 256
 GELU_A = math.sqrt(2.0 / math.pi)
 GELU_B = GELU_A * 0.044715
@@ -26,10 +28,10 @@
 def layer_kernel(
     dims,
     x_hbm, idx_hbm, gate_hbm, win_hbm, wout_hbm, sin_hbm, sout_hbm,
-    y_hbm,
+    y_ref,
     x_all, win, wout, idx_all, gate_all, disp, comb, rows_in, acc, hidden, rows_out,
-    part, sib_part, sib_fwd, link_out, link_in, y_buf, shared_h, shared_u,
-    small_sem, x_sem, win_sem, wout_sem, shared_sem, y_sem,
+    part, sib_part, sib_fwd, link_out, link_in, shared_h, shared_u,
+    fence_sem, small_sem, x_sem, win_sem, wout_sem, shared_sem,
     meta_send, meta_recv, xl_send, xl_recv, xs_send, xs_recv, xf_send, xf_recv,
     ps_send, ps_recv, pf_send, pf_recv, pl_send, pl_recv,
 ):
@@ -51,27 +53,27 @@
             src_ref=src, dst_ref=dst, send_sem=send, recv_sem=recv,
             device_id={'ep': dev}, device_id_type=MESH)
 
+    def fence():
+        pl.semaphore_signal(fence_sem, 1)
+        pl.semaphore_wait(fence_sem, 1)
+
     idx_cp = pltpu.make_async_copy(idx_hbm, idx_all.at[me], small_sem.at[0])
     gate_cp = pltpu.make_async_copy(gate_hbm, gate_all.at[me], small_sem.at[1])
-    idx_cp.start()
-    gate_cp.start()
     x_cps = [pltpu.make_async_copy(x_hbm.at[:, pl.ds(k * COLS, COLS)], x_all.at[k, rows_of(me)], x_sem.at[k]) for k in range(chunks)]
-    for cp in x_cps:
-        cp.start()
     win_cps = [pltpu.make_async_copy(win_hbm.at[:, pl.ds(k * COLS, COLS), :], win.at[k], win_sem.at[k]) for k in range(chunks)]
-    for cp in win_cps:
-        cp.start()
     wout_cps = [pltpu.make_async_copy(wout_hbm.at[:, :, pl.ds(n * COLS, COLS)], wout.at[n], wout_sem.at[n]) for n in range(chunks)]
-    for cp in wout_cps:
+    for cp in [idx_cp, gate_cp] + x_cps:
         cp.start()
 
     barrier = pltpu.get_barrier_semaphore()
     for peer in peers:
         pl.semaphore_signal(barrier, inc=1, device_id={'ep': peer}, device_id_type=MESH)
 
-    idx_cp.wait()
-    gate_cp.wait()
-    pl.semaphore_wait(barrier, 3)
+    with scope('w_small'):
+        for cp in [idx_cp, gate_cp] + x_cps:
+            cp.wait()
+    with scope('w_barrier'):
+        pl.semaphore_wait(barrier, 3)
     meta_cps = []
     for r, peer in enumerate(peers):
         meta_cps.append(remote(idx_all.at[me], idx_all.at[me], meta_send.at[r], meta_recv.at[r], peer))
@@ -85,12 +87,15 @@
         xs_cps.append(remote(mine, mine, xs_send.at[k], xs_recv.at[k], sib))
         xf_cps.append(remote(theirs, theirs, xf_send.at[k], xf_recv.at[k], sib))
     for k in range(chunks):
-        x_cps[k].wait()
         xl_cps[k].start()
         xs_cps[k].start()
-
-    for cp in meta_cps:
-        cp.wait_recv()
+    for cp in win_cps + wout_cps:
+        fence()
+        cp.start()
+
+    with scope('w_meta'):
+        for cp in meta_cps:
+            cp.wait_recv()
     group = tokens // tok
     idx_t = jnp.concatenate([idx_all[s] for s in range(group)], axis=1)
     gate_t = jnp.concatenate([gate_all[s] for s in range(group)], axis=1).astype(jnp.bfloat16).astype(jnp.float32)
@@ -112,19 +117,36 @@
     for i in range(local_e * slot // 256):
         comb[:, pl.ds(i * 256, 256)] = rows_out[pl.ds(i * 256, 256), :].T
 
-    xl_cps[0].wait_recv()
-    xf_cps[0].start()
-    for k in range(chunks):
+    def forward(k):
+        with scope(f'w_xl{k}'):
+            xl_cps[k].wait_recv()
+        xf_cps[k].start()
+
+    def await_rows(k):
+        with scope(f'w_xs{k}'):
+            xs_cps[k].wait_recv()
+        with scope(f'w_xf{k}'):
+            xf_cps[k].wait_recv()
+
+    def gather(k):
+        rows_in[k % 2] = dot(disp[...], x_all[k]).astype(jnp.bfloat16)
+
+    forward(0)
+    forward(1)
+    await_rows(0)
+    gather(0)
+    for k in range(chunks):
+        if k + 2 < chunks:
+            forward(k + 2)
         if k + 1 < chunks:
-            xl_cps[k + 1].wait_recv()
-            xf_cps[k + 1].start()
-        xs_cps[k].wait_recv()
-        xf_cps[k].wait_recv()
-        rows_in[...] = dot(disp[...], x_all[k]).astype(jnp.bfloat16)
-        win_cps[k].wait()
+            await_rows(k + 1)
+        with scope(f'w_win{k}'):
+            win_cps[k].wait()
+        if k + 1 < chunks:
+            gather(k + 1)
         for e in range(local_e):
             r = pl.ds(e * slot, slot)
-            term = dot(rows_in[r, :], win[k, e])
+            term = dot(rows_in[k % 2, r, :], win[k, e])
             if k == 0:
                 acc[r, :] = term
             elif k + 1 < chunks:
@@ -149,24 +171,34 @@
     pl_cps = [remote(link_out.at[n], link_in.at[n], pl_send.at[n], pl_recv.at[n], mir) for n in range(chunks)]
 
     def send_back(n):
-        pf_cps[n].wait_recv()
+        with scope(f'w_pf{n}'):
+            pf_cps[n].wait_recv()
         link_out[n] = part[n, rows_of(mir), :] + sib_fwd[n]
         pl_cps[n].start()
 
     for n in range(chunks):
-        wout_cps[n].wait()
+        with scope(f'w_wout{n}'):
+            wout_cps[n].wait()
+        total = None
+        done = 0
         for e in range(local_e):
             r = pl.ds(e * slot, slot)
             rows_out[r, :] = dot(hidden[r, :], wout[n, e]).astype(jnp.bfloat16)
-        part[n] = dot(comb[...], rows_out[...])
+            while done + 256 <= e * slot or (e + 1 == local_e and done < local_e * slot):
+                c = pl.ds(done, 256)
+                term = dot(comb[:, c], rows_out[c, :])
+                total = term if total is None else total + term
+                done += 256
+        part[n] = total
         pf_cps[n].start()
         ps_cps[n].start()
         if n:
             send_back(n - 1)
     send_back(chunks - 1)
 
-    for cp in shared_cps:
-        cp.wait()
+    with scope('w_shared'):
+        for cp in shared_cps:
+            cp.wait()
     for j in range(2):
         s = dot(x_all[0, rows_of(me), :], win[0, j])
         for k in range(1, chunks):
@@ -178,17 +210,16 @@
             u = u + dot(shared_h[:, pl.ds(i * COLS, COLS)], win[i, 2 + j])
         shared_u[:, pl.ds(j * ff, ff)] = u
 
-    y_cps = [pltpu.make_async_copy(y_buf.at[n], y_hbm.at[:, pl.ds(n * COLS, COLS)], y_sem.at[n]) for n in range(chunks)]
     for n in range(chunks):
-        ps_cps[n].wait_recv()
+        with scope(f'w_ps{n}'):
+            ps_cps[n].wait_recv()
         mine = shared_u[:, pl.ds(n * COLS, COLS)] + part[n, rows_of(me), :] + sib_part[n]
-        pl_cps[n].wait_recv()
-        y_buf[n] = (mine + link_in[n]).astype(jnp.bfloat16)
-        y_cps[n].start()
-    for cp in meta_cps + xl_cps + xs_cps + xf_cps + ps_cps + pf_cps + pl_cps:
-        cp.wait_send()
-    for cp in y_cps:
-        cp.wait()
+        with scope(f'w_pl{n}'):
+            pl_cps[n].wait_recv()
+        y_ref[:, pl.ds(n * COLS, COLS)] = (mine + link_in[n]).astype(jnp.bfloat16)
+    with scope('w_sends'):
+        for cp in meta_cps + xl_cps + xs_cps + xf_cps + ps_cps + pf_cps + pl_cps:
+            cp.wait_send()
 
 
 def solution(mesh):
@@ -213,7 +244,7 @@
             pltpu.VMEM((group, top_k, tok), f32),
             pltpu.VMEM((total, tokens), bf16),
             pltpu.VMEM((tokens, total), bf16),
-            pltpu.VMEM((total, COLS), bf16),
+            pltpu.VMEM((2, total, COLS), bf16),
             pltpu.VMEM((total, ff), f32),
             pltpu.VMEM((total, ff), bf16),
             pltpu.VMEM((total, COLS), bf16),
@@ -222,21 +253,20 @@
             pltpu.VMEM((chunks, tok, COLS), f32),
             pltpu.VMEM((chunks, tok, COLS), f32),
             pltpu.VMEM((chunks, tok, COLS), f32),
-            pltpu.VMEM((chunks, tok, COLS), bf16),
             pltpu.VMEM((tok, fs), bf16),
             pltpu.VMEM((tok, d_model), f32),
-            dma((2,)), dma((chunks,)), dma((chunks,)), dma((chunks,)), dma((24,)), dma((chunks,)),
+            pltpu.SemaphoreType.REGULAR, dma((2,)), dma((chunks,)), dma((chunks,)), dma((chunks,)), dma((24,)),
             dma((6,)), dma((6,)),
         ] + [dma((chunks,))] * 12
-        any_spec = pl.BlockSpec(memory_space=pl.ANY)
+        any_spec = pl.BlockSpec(memory_space=pltpu.HBM)
         return pl.pallas_call(
             functools.partial(layer_kernel, (tok, top_k, local_e, slot, tokens)),
-            out_shape=jax.ShapeDtypeStruct((tok, d_model), bf16),
+            out_shape=pltpu.VMEM((tok, d_model), bf16),
             in_specs=[any_spec] * 7,
-            out_specs=any_spec,
+            out_specs=pl.BlockSpec(memory_space=pltpu.VMEM),
             scratch_shapes=scratch,
             compiler_params=pltpu.CompilerParams(
-                collective_id=0, has_side_effects=True, vmem_limit_bytes=67043328),
+                collective_id=0, has_side_effects=True, vmem_limit_bytes=VMEM_LIMIT),
         )(x_loc, idx_loc.T, gate_loc.T, w_in, w_out, shared_in, shared_out)
 
     tok_spec = P(('dp', 'ep'), None)

time: 42.5 us -> 29.6 us (0.70)
  Pallas kernels: 40.7 us -> 28.7 us
  local copies, waits for them, and re-layouts: 1.62 us -> 0.68 us
    pallas_call x1, Pallas kernels: 40.7 us -> 28.7 us  [local_layer(): pl.pallas_call(functools.partial(layer_kernel, (tok, top_k, local_e, slot...]
    unnamed x1, local copies, waits for them, and re-layouts: 1.62 us -> 0.68 us
where the time goes in v2:
time: 29.6 us; the launch traced here: 29.4 us
  Pallas kernels  28.7 us (97%)
  local copies, waits for them, and re-layouts  0.68 us (2%)
    pallas_call x1, Pallas kernels, local_layer(): pl.pallas_call(functools.partial(layer_kernel, (tok, top_k, local_e, slot...  28.7 us
    unnamed x1, local copies, waits for them, and re-layouts  0.68 us

profile of v2, /device:TPU:0, one launch (start us, length us, event | category | flops | bytes accessed | tf_op | source)
XLA Modules:
  0.0 29.4 jit_solution(11189654858825199848)
XLA Ops:
  0.0 28.7 %shard_map.73 = bf16[64,1536]{1,0:T(8,128)(2,1)S(1)} custom-call(bf16[64,1536]{1,0:T(8,128)(2,1)} %x_hbm.1, s32[6,64]{1,0:T(8,128)} %bitcast.2, f32[6,64]{1,0:T(8,128)} %bitcast.3, bf16[16,1536,512]{2,1,0:T(8,128)(2,1)} %win_hbm.1, bf16[16,512,1536]{2,1,0:T(8,128)(2,1)} %wout_hbm.1, bf16[1536,1024]{1,0:T(8,128)(2,1)} %sin_hbm.1, bf16[1024,1536]{1,0:T(8,128)(2,1)} %sout_hbm.1), custom_call_target="tpu_custom_call" | custom-call | tf_op jit(solution)/shard_map/pallas_call | solution.py:262
  28.7 0.7 %copy.9 = bf16[64,1536]{1,0:T(8,128)(2,1)} copy(bf16[64,1536]{1,0:T(8,128)(2,1)S(1)} %shard_map.73) | data formatting | bytes 393216

commit v3 on v2

--- a/solution.py
+++ b/solution.py
@@ -128,13 +128,16 @@
         with scope(f'w_xf{k}'):
             xf_cps[k].wait_recv()
 
-    def gather(k):
-        rows_in[k % 2] = dot(disp[...], x_all[k]).astype(jnp.bfloat16)
+    def gather(k, piece, pieces):
+        m = local_e * slot // pieces
+        r = pl.ds(piece * m, m)
+        rows_in[k % 2, r, :] = dot(disp[r, :], x_all[k]).astype(jnp.bfloat16)
 
     forward(0)
     forward(1)
     await_rows(0)
-    gather(0)
+    gather(0, 0, 2)
+    gather(0, 1, 2)
     for k in range(chunks):
         if k + 2 < chunks:
             forward(k + 2)
@@ -142,29 +145,36 @@
             await_rows(k + 1)
         with scope(f'w_win{k}'):
             win_cps[k].wait()
-        if k + 1 < chunks:
-            gather(k + 1)
+        if k + 1 == chunks:
+            with scope('w_wout0'):
+                wout_cps[0].wait()
         for e in range(local_e):
             r = pl.ds(e * slot, slot)
-            term = dot(rows_in[k % 2, r, :], win[k, e])
-            if k == 0:
-                acc[r, :] = term
-            elif k + 1 < chunks:
-                acc[r, :] = acc[r, :] + term
-            else:
-                hidden[r, :] = gelu(acc[r, :] + term).astype(jnp.bfloat16)
+            for h in range(1):
+                c = pl.ds(h * (ff // 1), ff // 1)
+                term = dot(rows_in[k % 2, r, :], win[k, e, :, c])
+                if k == 0:
+                    acc[r, c] = term
+                elif k + 1 < chunks:
+                    acc[r, c] = acc[r, c] + term
+                else:
+                    hidden[r, c] = gelu(acc[r, c] + term).astype(jnp.bfloat16)
+            if k + 1 < chunks and e in [0,2,4,6,8,10,12,13]:
+                gather(k + 1, [0,2,4,6,8,10,12,13].index(e), len([0,2,4,6,8,10,12,13]))
 
     shared_cps = []
-    for k in range(chunks):
-        for j in range(2):
-            shared_cps.append(pltpu.make_async_copy(
-                sin_hbm.at[pl.ds(k * COLS, COLS), pl.ds(j * ff, ff)], win.at[k, j], shared_sem.at[k * 2 + j]))
-    for i in range(4):
-        for j in range(3):
-            shared_cps.append(pltpu.make_async_copy(
-                sout_hbm.at[pl.ds(i * COLS, COLS), pl.ds(j * ff, ff)], win.at[i, 2 + j], shared_sem.at[12 + i * 3 + j]))
-    for cp in shared_cps:
-        cp.start()
+
+    def load_shared():
+        for k in range(chunks):
+            for j in range(2):
+                shared_cps.append(pltpu.make_async_copy(
+                    sin_hbm.at[pl.ds(k * COLS, COLS), pl.ds(j * ff, ff)], win.at[k, j], shared_sem.at[k * 2 + j]))
+        for i in range(4):
+            for j in range(3):
+                shared_cps.append(pltpu.make_async_copy(
+                    sout_hbm.at[pl.ds(i * COLS, COLS), pl.ds(j * ff, ff)], win.at[i, 2 + j], shared_sem.at[12 + i * 3 + j]))
+        for cp in shared_cps:
+            cp.start()
 
     ps_cps = [remote(part.at[n, rows_of(sib)], sib_part.at[n], ps_send.at[n], ps_recv.at[n], sib) for n in range(chunks)]
     pf_cps = [remote(part.at[n, rows_of(diag)], sib_fwd.at[n], pf_send.at[n], pf_recv.at[n], sib) for n in range(chunks)]
@@ -177,8 +187,9 @@
         pl_cps[n].start()
 
     for n in range(chunks):
-        with scope(f'w_wout{n}'):
-            wout_cps[n].wait()
+        if n:
+            with scope(f'w_wout{n}'):
+                wout_cps[n].wait()
         total = None
         done = 0
         for e in range(local_e):
@@ -192,6 +203,8 @@
         part[n] = total
         pf_cps[n].start()
         ps_cps[n].start()
+        if n == 0:
+            load_shared()
         if n:
             send_back(n - 1)
     send_back(chunks - 1)

time: 29.6 us -> 28.8 us (0.973)
  Pallas kernels: 28.7 us -> 27.9 us
    pallas_call x1, Pallas kernels: 28.7 us -> 27.9 us  [local_layer(): pl.pallas_call(functools.partial(layer_kernel, (tok, top_k, local_e, slot...]
where the time goes in v3:
time: 28.8 us; the launch traced here: 28.6 us
  Pallas kernels  27.9 us (97%)
  local copies, waits for them, and re-layouts  0.68 us (2%)
    pallas_call x1, Pallas kernels, local_layer(): pl.pallas_call(functools.partial(layer_kernel, (tok, top_k, local_e, slot...  27.9 us
    unnamed x1, local copies, waits for them, and re-layouts  0.68 us

profile of v3, /device:TPU:0, one launch (start us, length us, event | category | flops | bytes accessed | tf_op | source)
XLA Modules:
  0.0 28.6 jit_solution(2312486886539278698)
XLA Ops:
  0.0 27.9 %shard_map.73 = bf16[64,1536]{1,0:T(8,128)(2,1)S(1)} custom-call(bf16[64,1536]{1,0:T(8,128)(2,1)} %x_hbm.1, s32[6,64]{1,0:T(8,128)} %bitcast.2, f32[6,64]{1,0:T(8,128)} %bitcast.3, bf16[16,1536,512]{2,1,0:T(8,128)(2,1)} %win_hbm.1, bf16[16,512,1536]{2,1,0:T(8,128)(2,1)} %wout_hbm.1, bf16[1536,1024]{1,0:T(8,128)(2,1)} %sin_hbm.1, bf16[1024,1536]{1,0:T(8,128)(2,1)} %sout_hbm.1), custom_call_target="tpu_custom_call" | custom-call | tf_op jit(solution)/shard_map/pallas_call | solution.py:275
  27.9 0.7 %copy.9 = bf16[64,1536]{1,0:T(8,128)(2,1)} copy(bf16[64,1536]{1,0:T(8,128)(2,1)S(1)} %shard_map.73) | data formatting | bytes 393216

commit v4 on v3

--- a/solution.py
+++ b/solution.py
@@ -10,6 +10,8 @@
 
 MESH = pl.DeviceIdType.MESH
 LOAD_MULT = 3
+SPOTS = (0, 2, 4, 6, 8, 10, 12, 13)
+LAG = 2
 VMEM_LIMIT = 61500000
 scope = jax.named_scope
 COLS = 256
@@ -31,10 +33,10 @@
     y_ref,
     x_all, win, wout, idx_all, gate_all, disp, comb, rows_in, acc, hidden, rows_out,
     part, sib_part, sib_fwd, link_out, link_in, shared_h, shared_u,
-    fence_sem, small_sem, x_sem, win_sem, wout_sem, shared_sem,
-    meta_send, meta_recv, xl_send, xl_recv, xs_send, xs_recv, xf_send, xf_recv,
-    ps_send, ps_recv, pf_send, pf_recv, pl_send, pl_recv,
-):
+    *sems):
+    (fence_sem, small_sem, x_sem, win_sem, wout_sem, shared_sem,
+     meta_send, meta_recv, xl_send, xl_recv, xs_send, xs_recv, xf_send, xf_recv,
+     ps_send, ps_recv, pf_send, pf_recv, pl_send, pl_recv) = sems
     tok, top_k, local_e, slot, tokens = dims
     d_model, ff = win_hbm.shape[1], win_hbm.shape[2]
     chunks = d_model // COLS
@@ -138,6 +140,26 @@
     await_rows(0)
     gather(0, 0, 2)
     gather(0, 1, 2)
+    def first(k, e):
+        r = pl.ds(e * slot, slot)
+        term = dot(rows_in[k % 2, r, :], win[k, e])
+        if k == 0:
+            acc[r, :] = term
+        elif k + 1 < chunks:
+            acc[r, :] = acc[r, :] + term
+        else:
+            hidden[r, :] = gelu(acc[r, :] + term).astype(jnp.bfloat16)
+
+    def second(n, e, total):
+        r = pl.ds(e * slot, slot)
+        rows_out[r, :] = dot(hidden[r, :], wout[n, e]).astype(jnp.bfloat16)
+        ready = e * slot // COLS if e + 1 < local_e else local_e * slot // COLS
+        for i in range(max(e - 1, 0) * slot // COLS, ready):
+            c = pl.ds(i * COLS, COLS)
+            term = dot(comb[:, c], rows_out[c, :])
+            total = term if total is None else total + term
+        return total
+
     for k in range(chunks):
         if k + 2 < chunks:
             forward(k + 2)
@@ -145,34 +167,28 @@
             await_rows(k + 1)
         with scope(f'w_win{k}'):
             win_cps[k].wait()
-        if k + 1 == chunks:
-            with scope('w_wout0'):
-                wout_cps[0].wait()
-        for e in range(local_e):
-            r = pl.ds(e * slot, slot)
-            for h in range(1):
-                c = pl.ds(h * (ff // 1), ff // 1)
-                term = dot(rows_in[k % 2, r, :], win[k, e, :, c])
-                if k == 0:
-                    acc[r, c] = term
-                elif k + 1 < chunks:
-                    acc[r, c] = acc[r, c] + term
-                else:
-                    hidden[r, c] = gelu(acc[r, c] + term).astype(jnp.bfloat16)
-            if k + 1 < chunks and e in [0,2,4,6,8,10,12,13]:
-                gather(k + 1, [0,2,4,6,8,10,12,13].index(e), len([0,2,4,6,8,10,12,13]))
+        if k + 1 < chunks:
+            for e in range(local_e):
+                first(k, e)
+                if e in SPOTS:
+                    gather(k + 1, SPOTS.index(e), len(SPOTS))
+    with scope('w_wout0'):
+        wout_cps[0].wait()
+    total = None
+    for e in range(local_e + LAG):
+        if e < local_e:
+            first(chunks - 1, e)
+        if e >= LAG:
+            total = second(0, e - LAG, total)
 
     shared_cps = []
 
     def load_shared():
-        for k in range(chunks):
-            for j in range(2):
-                shared_cps.append(pltpu.make_async_copy(
-                    sin_hbm.at[pl.ds(k * COLS, COLS), pl.ds(j * ff, ff)], win.at[k, j], shared_sem.at[k * 2 + j]))
-        for i in range(4):
-            for j in range(3):
-                shared_cps.append(pltpu.make_async_copy(
-                    sout_hbm.at[pl.ds(i * COLS, COLS), pl.ds(j * ff, ff)], win.at[i, 2 + j], shared_sem.at[12 + i * 3 + j]))
+        for j in range(2):
+            shared_cps.append(pltpu.make_async_copy(sin_hbm.at[:, :, pl.ds(j * ff, ff)], win.at[:, j], shared_sem.at[j]))
+        for j in range(3):
+            shared_cps.append(pltpu.make_async_copy(
+                sout_hbm.at[:, :, pl.ds(j * ff, ff)], win.at[pl.ds(0, sout_hbm.shape[0]), 2 + j], shared_sem.at[2 + j]))
         for cp in shared_cps:
             cp.start()
 
@@ -190,16 +206,10 @@
         if n:
             with scope(f'w_wout{n}'):
                 wout_cps[n].wait()
-        total = None
-        done = 0
-        for e in range(local_e):
-            r = pl.ds(e * slot, slot)
-            rows_out[r, :] = dot(hidden[r, :], wout[n, e]).astype(jnp.bfloat16)
-            while done + 256 <= e * slot or (e + 1 == local_e and done < local_e * slot):
-                c = pl.ds(done, 256)
-                term = dot(comb[:, c], rows_out[c, :])
-                total = term if total is None else total + term
-                done += 256
+        if n:
+            total = None
+            for e in range(local_e):
+                total = second(n, e, total)
         part[n] = total
         pf_cps[n].start()
         ps_cps[n].start()
@@ -268,19 +278,24 @@
             pltpu.VMEM((chunks, tok, COLS), f32),
             pltpu.VMEM((tok, fs), bf16),
             pltpu.VMEM((tok, d_model), f32),
-            pltpu.SemaphoreType.REGULAR, dma((2,)), dma((chunks,)), dma((chunks,)), dma((chunks,)), dma((24,)),
-            dma((6,)), dma((6,)),
-        ] + [dma((chunks,))] * 12
+        ]
+        sems = [pltpu.SemaphoreType.REGULAR, dma((2,)), dma((chunks,)), dma((chunks,)), dma((chunks,)), dma((5,)), dma((6,)), dma((6,))]
+        sems += [dma((chunks,))] * 12
+
+        def kernel(*refs):
+            pl.run_scoped(functools.partial(layer_kernel, (tok, top_k, local_e, slot, tokens), *refs), *sems)
+
         any_spec = pl.BlockSpec(memory_space=pltpu.HBM)
         return pl.pallas_call(
-            functools.partial(layer_kernel, (tok, top_k, local_e, slot, tokens)),
+            kernel,
             out_shape=pltpu.VMEM((tok, d_model), bf16),
             in_specs=[any_spec] * 7,
             out_specs=pl.BlockSpec(memory_space=pltpu.VMEM),
             scratch_shapes=scratch,
             compiler_params=pltpu.CompilerParams(
                 collective_id=0, has_side_effects=True, vmem_limit_bytes=VMEM_LIMIT),
-        )(x_loc, idx_loc.T, gate_loc.T, w_in, w_out, shared_in, shared_out)
+        )(x_loc, idx_loc.T, gate_loc.T, w_in, w_out,
+          shared_in.reshape(chunks, COLS, fs), shared_out.reshape(fs // COLS, COLS, d_model))
 
     tok_spec = P(('dp', 'ep'), None)
     expert_spec = P('ep', None, None)

time: 28.8 us -> 27.5 us (0.955)
  Pallas kernels: 27.9 us -> 26.7 us
    pallas_call x1, Pallas kernels: 27.9 us -> 26.7 us  [local_layer(): pl.pallas_call(kernel, out_shape=pltpu.VMEM((tok, d_model), bf16), in_spe...]
where the time goes in v4:
time: 27.5 us; the launch traced here: 27.4 us
  Pallas kernels  26.7 us (97%)
  local copies, waits for them, and re-layouts  0.68 us (2%)
    pallas_call x1, Pallas kernels, local_layer(): pl.pallas_call(kernel, out_shape=pltpu.VMEM((tok, d_model), bf16), in_spe...  26.7 us
    unnamed x1, local copies, waits for them, and re-layouts  0.68 us

profile of v4, /device:TPU:0, one launch (start us, length us, event | category | flops | bytes accessed | tf_op | source)
XLA Modules:
  0.0 27.4 jit_solution(6113111266924433731)
XLA Ops:
  0.0 26.7 %shard_map.73 = bf16[64,1536]{1,0:T(8,128)(2,1)S(1)} custom-call(bf16[64,1536]{1,0:T(8,128)(2,1)} %refs_0_.1, s32[6,64]{1,0:T(8,128)} %bitcast.6, f32[6,64]{1,0:T(8,128)} %bitcast.7, bf16[16,1536,512]{2,1,0:T(8,128)(2,1)} %refs_3_.1, bf16[16,512,1536]{2,1,0:T(8,128)(2,1)} %refs_4_.1, bf16[6,256,1024]{2,1,0:T(8,128)(2,1)} %bitcast.4, ...), custom_call_target="tpu_custom_call" | custom-call | tf_op jit(solution)/shard_map/pallas_call | solution.py:289
  26.7 0.7 %copy.9 = bf16[64,1536]{1,0:T(8,128)(2,1)} copy(bf16[64,1536]{1,0:T(8,128)(2,1)S(1)} %shard_map.73) | data formatting | bytes 393216
